TPU v7x, 32 devices: a whole 2x2x4 slice. The times are simulated.
32 devices in a mesh: py: 8 (over z, x), px: 4 (over y, core).
Axes of the slice: x: 2, y: 2, z: 4, core: 2. Of those that a mesh axis runs over, the one named last changes fastest.
Arguments:
- density: float32 [256, 128, 128], P('py', 'px'), may hold values from 0.5 to 2
- conductance: float32 [256, 128, 128], P('py', 'px'), may hold values from 0.03 to 0.22
- source: float32 [256, 128, 128], P('py', 'px'), may hold values from -0.2 to 0.2
Outputs:
- anomaly: float32 [256, 128, 128], P('py', 'px')
- density_end: float32 [256, 128, 128], P('py', 'px')
All inputs are finite; a program needn't handle non-finite values.
Results may differ from a plain program's by a relative error of at most 0.00002.
Values sent between devices are 32-bit elements; how exact they have to be, the bound alone decides.
No kernel may reach another device: no remote copies, remote signals or barrier semaphores. Data moves between devices by JAX's collectives and lax.ppermute only.
A program may use at most 64 MiB of HBM per device.

v0:
```python
import jax
import jax.numpy as jnp
from jax import lax
from jax.sharding import PartitionSpec as P

STEPS = 6


def with_halo(cells, sides, width):
    for axis, dim in sides:
        count = lax.axis_size(axis)
        ends = count - 1
        head = lax.slice_in_dim(cells, 0, width, axis=dim)
        tail = lax.slice_in_dim(cells, cells.shape[dim] - width, cells.shape[dim], axis=dim)
        cells = jnp.concatenate(
            [
                lax.ppermute(tail, axis, [(i, (i + 1) % count) for i in range(ends)]),
                cells,
                lax.ppermute(head, axis, [((i + 1) % count, i) for i in range(ends)]),
            ],
            axis=dim,
        )
    return cells


def strip_edges(values, dims):
    for dim in dims:
        values = lax.slice_in_dim(values, 1, values.shape[dim] - 1, axis=dim)
    return values


def neighbour(values, dim, start, dims):
    others = [other for other in dims if other != dim]
    values = strip_edges(values, others)
    return lax.slice_in_dim(values, start, start + values.shape[dim] - 2, axis=dim)


def one_step(padded, conductance, source):
    middle = strip_edges(padded, (0, 1))
    lower = [neighbour(padded, dim, 0, (0, 1)) for dim in (0, 1)]
    upper = [neighbour(padded, dim, 2, (0, 1)) for dim in (0, 1)]
    spread = lower[0] + upper[0] + lower[1] + upper[1] - 4.0 * middle
    return middle + conductance * spread + source


def per_device(density, conductance, source):
    padded = with_halo(density, (("py", 0), ("px", 1)), STEPS)
    wide_parts = with_halo(
        jnp.concatenate([conductance, source], axis=2), (("py", 0), ("px", 1)), STEPS - 1
    )
    wide_conductance, wide_source = jnp.split(wide_parts, 2, axis=2)
    for step in range(STEPS):
        later = one_step(padded, wide_conductance, wide_source)
        values = later
        margin = STEPS - 1 - step
        place = lax.axis_index("py") * density.shape[0] - margin + jnp.arange(values.shape[0])
        keep_cells = (place >= 0) & (place < density.shape[0] * lax.axis_size("py"))
        values = jnp.where(keep_cells.reshape((-1,) + (1,) * 2), values, 0.0)
        place = lax.axis_index("px") * density.shape[1] - margin + jnp.arange(values.shape[1])
        keep_cells = (place >= 0) & (place < density.shape[1] * lax.axis_size("px"))
        values = jnp.where(keep_cells.reshape((-1,) + (1,) * 1), values, 0.0)
        later = values
        if step < STEPS - 1:
            wide_conductance = strip_edges(wide_conductance, (0, 1))
            wide_source = strip_edges(wide_source, (0, 1))
        padded = later
    density = padded
    count = density.shape[0] * lax.axis_size("py")
    line_mean = lax.psum(jnp.sum(density, axis=0, keepdims=True), "py") / count
    centred = density - line_mean
    line_variance = lax.psum(jnp.sum(centred * centred, axis=0, keepdims=True), "py") / count
    anomaly = centred * lax.rsqrt(line_variance + 0.0001)
    return (anomaly, density)


def solution(mesh):
    in_specs = (P("py", "px", None), P("py", "px", None), P("py", "px", None))
    out_specs = (P("py", "px", None), P("py", "px", None))
    return jax.shard_map(
        per_device, mesh=mesh, in_specs=in_specs, out_specs=out_specs, check_vma=False
    )
```

profile of v0, /device:TPU:4, one launch (start us, length us, event | category | flops | bytes accessed | tf_op | source)
XLA Modules:
  0.0 108.5 jit_solution(7742609945512522112)
XLA Ops:
  0.6 0.0 copy-start.3
  0.6 1.1 %constant_dynamic-update-slice_fusion.4 = f32[32,32,256]{2,1,0:T(8,128)S(1)} fusion(f32[32,32,128]{2,1,0:T(8,128)} %param.4), kind=kLoop, calls=%fused_computation.67 | loop fusion | bytes 1048576
  1.8 1.1 constant_dynamic-update-slice_fusion.3
  2.9 1.3 %collective-permute-start.5 = (f32[5,32,256]{2,1,0:T(8,128)S(1)}, f32[5,32,256]{2,1,0:T(8,128)S(1)}, u32[]{:S(2)}, u32[]{:S(2)}) collective-permute-start(f32[5,32,256]{2,1,0:T(8,128)S(1)} %get-tuple-element.7), channel_id=1, source_target_pairs={{4,0},{8,4},{12,8},{16,12},{20,16},{24,20},{28,24},{5,1},{9,5},{13... | collective-permute-start | bytes 491528 | tf_op jit(solution)/shard_map/ppermute | solution.py:19
  4.2 4.6 %collective-permute-start.4 = (f32[5,32,256]{2,1,0:T(8,128)S(1)}, f32[5,32,256]{2,1,0:T(8,128)S(1)}, u32[]{:S(2)}, u32[]{:S(2)}) collective-permute-start(f32[5,32,256]{2,1,0:T(8,128)S(1)} %get-tuple-element.6), channel_id=1, source_target_pairs={{0,4},{4,8},{8,12},{12,16},{16,20},{20,24},{24,28},{1,5},{5,9},{9,... | collective-permute-start | bytes 491528 | tf_op jit(solution)/shard_map/ppermute | solution.py:17
  8.8 0.0 copy-done.3
  8.8 4.3 %collective-permute-start = (f32[6,32,128]{2,1,0:T(8,128)S(1)}, f32[6,32,128]{2,1,0:T(8,128)S(1)}, u32[]{:S(2)}, u32[]{:S(2)}) collective-permute-start(f32[6,32,128]{2,1,0:T(8,128)S(1)} %get-tuple-element.11), channel_id=1, source_target_pairs={{0,4},{4,8},{8,12},{12,16},{16,20},{20,24},{24,28},{1,5},{5,9},{9,... | collective-permute-start | bytes 294920 | tf_op jit(solution)/shard_map/ppermute | solution.py:17
  13.1 1.3 %collective-permute-start.1 = (f32[6,32,128]{2,1,0:T(8,128)S(1)}, f32[6,32,128]{2,1,0:T(8,128)S(1)}, u32[]{:S(2)}, u32[]{:S(2)}) collective-permute-start(f32[6,32,128]{2,1,0:T(8,128)S(1)} %get-tuple-element.10), channel_id=1, source_target_pairs={{4,0},{8,4},{12,8},{16,12},{20,16},{24,20},{28,24},{5,1},{9,5},{13... | collective-permute-start | bytes 294920 | tf_op jit(solution)/shard_map/ppermute | solution.py:19
  14.5 2.9 %collective-permute-done = f32[6,32,128]{2,1,0:T(8,128)S(1)} collective-permute-done((f32[6,32,128]{2,1,0:T(8,128)S(1)}, f32[6,32,128]{2,1,0:T(8,128)S(1)}, u32[]{:S(2)}, u32[]{:S(2)}) %collective-permute-start) | collective-permute-done | bytes 98336 | tf_op jit(solution)/shard_map/ppermute | solution.py:17
  17.4 2.2 %collective-permute-done.1 = f32[6,32,128]{2,1,0:T(8,128)S(1)} collective-permute-done((f32[6,32,128]{2,1,0:T(8,128)S(1)}, f32[6,32,128]{2,1,0:T(8,128)S(1)}, u32[]{:S(2)}, u32[]{:S(2)}) %collective-permute-start.1) | collective-permute-done | bytes 98336 | tf_op jit(solution)/shard_map/ppermute | solution.py:19
  19.7 1.9 %collective-permute-start.3 = (f32[44,6,128]{2,1,0:T(8,128)S(1)}, f32[44,6,128]{2,1,0:T(8,128)S(1)}, u32[]{:S(2)}, u32[]{:S(2)}) collective-permute-start(f32[44,6,128]{2,1,0:T(8,128)S(1)} %get-tuple-element.9), channel_id=1, source_target_pairs={{1,0},{2,1},{3,2},{5,4},{6,5},{7,6},{9,8},{10,9},{11,10},{13,12},{... | collective-permute-start | bytes 405512 | tf_op jit(solution)/shard_map/ppermute | solution.py:19
  21.6 2.4 %collective-permute-start.2 = (f32[44,6,128]{2,1,0:T(8,128)S(1)}, f32[44,6,128]{2,1,0:T(8,128)S(1)}, u32[]{:S(2)}, u32[]{:S(2)}) collective-permute-start(f32[44,6,128]{2,1,0:T(8,128)S(1)} %get-tuple-element.8), channel_id=1, source_target_pairs={{0,1},{1,2},{2,3},{4,5},{5,6},{6,7},{8,9},{9,10},{10,11},{12,13},{... | collective-permute-start | bytes 405512 | tf_op jit(solution)/shard_map/ppermute | solution.py:17
  24.0 0.0 collective-permute-done.5
  24.0 0.0 collective-permute-done.4
  24.0 0.1 pad_maximum_fusion.4
  24.1 3.1 %collective-permute-start.7 = (f32[42,5,256]{2,1,0:T(8,128)S(1)}, f32[42,5,256]{2,1,0:T(8,128)S(1)}, u32[]{:S(2)}, u32[]{:S(2)}) collective-permute-start(f32[42,5,256]{2,1,0:T(8,128)S(1)} %get-tuple-element.5), channel_id=1, source_target_pairs={{1,0},{2,1},{3,2},{5,4},{6,5},{7,6},{9,8},{10,9},{11,10},{13,12},{... | collective-permute-start | bytes 645128 | tf_op jit(solution)/shard_map/ppermute | solution.py:19
  27.3 1.9 %collective-permute-start.6 = (f32[42,5,256]{2,1,0:T(8,128)S(1)}, f32[42,5,256]{2,1,0:T(8,128)S(1)}, u32[]{:S(2)}, u32[]{:S(2)}) collective-permute-start(f32[42,5,256]{2,1,0:T(8,128)S(1)} %get-tuple-element.4), channel_id=1, source_target_pairs={{0,1},{1,2},{2,3},{4,5},{5,6},{6,7},{8,9},{9,10},{10,11},{12,13},{... | collective-permute-start | bytes 645128 | tf_op jit(solution)/shard_map/ppermute | solution.py:17
  29.2 0.0 collective-permute-done.3
  29.2 0.0 collective-permute-done.2
  29.2 0.1 pad_maximum_fusion.1
  29.4 2.6 %collective-permute-done.7 = f32[42,5,256]{2,1,0:T(8,128)S(1)} collective-permute-done((f32[42,5,256]{2,1,0:T(8,128)S(1)}, f32[42,5,256]{2,1,0:T(8,128)S(1)}, u32[]{:S(2)}, u32[]{:S(2)}) %collective-permute-start.7) | collective-permute-done | bytes 215072 | tf_op jit(solution)/shard_map/ppermute | solution.py:19
  32.0 3.8 %collective-permute-done.6 = f32[42,5,256]{2,1,0:T(8,128)S(1)} collective-permute-done((f32[42,5,256]{2,1,0:T(8,128)S(1)}, f32[42,5,256]{2,1,0:T(8,128)S(1)}, u32[]{:S(2)}, u32[]{:S(2)}) %collective-permute-start.6) | collective-permute-done | bytes 215072 | tf_op jit(solution)/shard_map/ppermute | solution.py:17
  35.8 0.3 pad_maximum_fusion
  36.1 0.5 fusion.1
  36.7 0.5 fusion.6
  37.2 0.5 fusion.11
  37.7 0.5 fusion.16
  38.2 0.0 copy-start.1
  38.3 0.0 copy-start.2
  38.3 0.5 fusion.21
  38.7 0.5 copy-done.1
  39.3 0.2 copy-done.2
  39.4 0.3 fusion.31
  39.7 0.0 copy-start
  39.7 34.8 %psum.14 = f32[1,32,128]{2,1,0:T(8,128)S(1)} all-reduce(f32[1,32,128]{2,1,0:T(8,128)S(1)} %bitcast.6), channel_id=1, replica_groups=mesh['py'=8,'px'=4] {'py'}, use_global_device_ids=true, to_apply=%region_1.2 | all-reduce | flops 4096 | bytes 32768 | tf_op jit(solution)/shard_map/psum | solution.py:69
  74.5 0.1 multiply_reduce_fusion
  74.6 33.0 %psum.15 = f32[1,32,128]{2,1,0:T(8,128)S(1)} all-reduce(f32[1,32,128]{2,1,0:T(8,128)S(1)} %bitcast.7), channel_id=1, replica_groups=mesh['py'=8,'px'=4] {'py'}, use_global_device_ids=true, to_apply=%region_3.4 | all-reduce | flops 4096 | bytes 32768 | tf_op jit(solution)/shard_map/psum | solution.py:71
  107.6 0.9 subtract_multiply_fusion
  108.5 0.0 copy-done
  (14 shorter events, 0.2 us)
Async XLA Ops:
  0.6 8.1 %copy-start.3 = (f32[32,32,128]{2,1,0:T(8,128)S(1)}, f32[32,32,128]{2,1,0:T(8,128)}, u32[]{:S(2)}) copy-start(f32[32,32,128]{2,1,0:T(8,128)} %param.3) | copy-start | bytes 1572868
  2.9 21.1 %collective-permute-start.5 = (f32[5,32,256]{2,1,0:T(8,128)S(1)}, f32[5,32,256]{2,1,0:T(8,128)S(1)}, u32[]{:S(2)}, u32[]{:S(2)}) collective-permute-start(f32[5,32,256]{2,1,0:T(8,128)S(1)} %get-tuple-element.7), channel_id=1, source_target_pairs={{4,0},{8,4},{12,8},{16,12},{20,16},{24,20},{28,24},{5,1},{9,5},{13... | collective-permute-start | bytes 491528 | tf_op jit(solution)/shard_map/ppermute | solution.py:19
  4.2 19.8 %collective-permute-start.4 = (f32[5,32,256]{2,1,0:T(8,128)S(1)}, f32[5,32,256]{2,1,0:T(8,128)S(1)}, u32[]{:S(2)}, u32[]{:S(2)}) collective-permute-start(f32[5,32,256]{2,1,0:T(8,128)S(1)} %get-tuple-element.6), channel_id=1, source_target_pairs={{0,4},{4,8},{8,12},{12,16},{16,20},{20,24},{24,28},{1,5},{5,9},{9,... | collective-permute-start | bytes 491528 | tf_op jit(solution)/shard_map/ppermute | solution.py:17
  8.8 8.5 %collective-permute-start = (f32[6,32,128]{2,1,0:T(8,128)S(1)}, f32[6,32,128]{2,1,0:T(8,128)S(1)}, u32[]{:S(2)}, u32[]{:S(2)}) collective-permute-start(f32[6,32,128]{2,1,0:T(8,128)S(1)} %get-tuple-element.11), channel_id=1, source_target_pairs={{0,4},{4,8},{8,12},{12,16},{16,20},{20,24},{24,28},{1,5},{5,9},{9,... | collective-permute-start | bytes 294920 | tf_op jit(solution)/shard_map/ppermute | solution.py:17
  13.1 6.5 %collective-permute-start.1 = (f32[6,32,128]{2,1,0:T(8,128)S(1)}, f32[6,32,128]{2,1,0:T(8,128)S(1)}, u32[]{:S(2)}, u32[]{:S(2)}) collective-permute-start(f32[6,32,128]{2,1,0:T(8,128)S(1)} %get-tuple-element.10), channel_id=1, source_target_pairs={{4,0},{8,4},{12,8},{16,12},{20,16},{24,20},{28,24},{5,1},{9,5},{13... | collective-permute-start | bytes 294920 | tf_op jit(solution)/shard_map/ppermute | solution.py:19
  19.7 9.5 %collective-permute-start.3 = (f32[44,6,128]{2,1,0:T(8,128)S(1)}, f32[44,6,128]{2,1,0:T(8,128)S(1)}, u32[]{:S(2)}, u32[]{:S(2)}) collective-permute-start(f32[44,6,128]{2,1,0:T(8,128)S(1)} %get-tuple-element.9), channel_id=1, source_target_pairs={{1,0},{2,1},{3,2},{5,4},{6,5},{7,6},{9,8},{10,9},{11,10},{13,12},{... | collective-permute-start | bytes 405512 | tf_op jit(solution)/shard_map/ppermute | solution.py:19
  21.6 7.6 %collective-permute-start.2 = (f32[44,6,128]{2,1,0:T(8,128)S(1)}, f32[44,6,128]{2,1,0:T(8,128)S(1)}, u32[]{:S(2)}, u32[]{:S(2)}) collective-permute-start(f32[44,6,128]{2,1,0:T(8,128)S(1)} %get-tuple-element.8), channel_id=1, source_target_pairs={{0,1},{1,2},{2,3},{4,5},{5,6},{6,7},{8,9},{9,10},{10,11},{12,13},{... | collective-permute-start | bytes 405512 | tf_op jit(solution)/shard_map/ppermute | solution.py:17
  24.1 7.9 %collective-permute-start.7 = (f32[42,5,256]{2,1,0:T(8,128)S(1)}, f32[42,5,256]{2,1,0:T(8,128)S(1)}, u32[]{:S(2)}, u32[]{:S(2)}) collective-permute-start(f32[42,5,256]{2,1,0:T(8,128)S(1)} %get-tuple-element.5), channel_id=1, source_target_pairs={{1,0},{2,1},{3,2},{5,4},{6,5},{7,6},{9,8},{10,9},{11,10},{13,12},{... | collective-permute-start | bytes 645128 | tf_op jit(solution)/shard_map/ppermute | solution.py:19
  27.3 8.6 %collective-permute-start.6 = (f32[42,5,256]{2,1,0:T(8,128)S(1)}, f32[42,5,256]{2,1,0:T(8,128)S(1)}, u32[]{:S(2)}, u32[]{:S(2)}) collective-permute-start(f32[42,5,256]{2,1,0:T(8,128)S(1)} %get-tuple-element.4), channel_id=1, source_target_pairs={{0,1},{1,2},{2,3},{4,5},{5,6},{6,7},{8,9},{9,10},{10,11},{12,13},{... | collective-permute-start | bytes 645128 | tf_op jit(solution)/shard_map/ppermute | solution.py:17
  38.2 1.0 copy-start.1
  38.3 1.2 %copy-start.2 = (f32[32,32,128]{2,1,0:T(8,128)S(1)}, f32[32,32,128]{2,1,0:T(8,128)}, u32[]{:S(2)}) copy-start(f32[32,32,128]{2,1,0:T(8,128)} %param.4) | copy-start | bytes 1572868
  39.7 68.7 %copy-start = (f32[32,32,128]{2,1,0:T(8,128)}, f32[32,32,128]{2,1,0:T(8,128)S(1)}, u32[]{:S(2)}) copy-start(f32[32,32,128]{2,1,0:T(8,128)S(1)} %get-tuple-element.3) | copy-start | bytes 1572868
where the time goes:
time: 109 us; the launch traced here: 108 us
  blocking collectives  67.8 us (62%)
  starting transfers between devices  20.8 us (19%)
  waiting for transfers between devices  11.5 us (11%)
  other arithmetic  4.37 us (4%)
  local copies, waits for them, and re-layouts  3.05 us (3%)
    psum x1, blocking collectives, per_device(): line_mean = lax.psum(jnp.sum(density, axis=0, keepdims=True), 'py') / count  34.8 us
    psum x1, blocking collectives, per_device(): lax.psum(jnp.sum(centred * centred, axis=0, keepdims=True), 'py') / count  33 us
    ppermute x4, starting transfers between devices, with_halo(): lax.ppermute(tail, axis, [(i, (i + 1) % count) for i in range(ends)])  13.2 us
    ppermute x4, starting transfers between devices, with_halo(): lax.ppermute(head, axis, [((i + 1) % count, i) for i in range(ends)])  7.65 us
    ppermute x4, waiting for transfers between devices, with_halo(): lax.ppermute(tail, axis, [(i, (i + 1) % count) for i in range(ends)])  6.68 us
    ppermute x4, waiting for transfers between devices, with_halo(): lax.ppermute(head, axis, [((i + 1) % count, i) for i in range(ends)])  4.86 us
    select_n x5, other arithmetic, per_device(): values = jnp.where(keep_cells.reshape((-1,) + (1,) * 1), values, 0.0)  2.55 us
  transfers between devices with their start and end apart: 8, of which 4 were waited for; matrix products, arithmetic and copies ran while one was open for 0% of the time, Pallas kernels for 0%

commit v1 on v0

v1 whole, which is shorter than its diff:
```python
import jax
import jax.numpy as jnp
from jax import lax
from jax.sharding import PartitionSpec as P

STEPS = 6


def exchange(to_upper, to_lower, axis):
    count = lax.axis_size(axis)
    up = [(i, i + 1) for i in range(count - 1)]
    down = [(i + 1, i) for i in range(count - 1)]
    return lax.ppermute(to_upper, axis, up), lax.ppermute(to_lower, axis, down)


def cut(values, start, stop, dim):
    return lax.slice_in_dim(values, start, stop, axis=dim)


def with_halo(density, conductance, source, axis, dim):
    deep, less = STEPS, STEPS - 1
    size = density.shape[dim]
    parts = (density, conductance, source)
    depths = (deep, less, less)
    tail = jnp.concatenate([cut(v, size - w, size, dim) for v, w in zip(parts, depths)], dim)
    head = jnp.concatenate([cut(v, 0, w, dim) for v, w in zip(parts, depths)], dim)
    lower, upper = exchange(tail, head, axis)
    wide, at = [], 0
    for v, w in zip(parts, depths):
        edge = deep - w
        pads = [(0, 0)] * v.ndim
        pads[dim] = (edge, edge)
        joined = jnp.concatenate([cut(lower, at, at + w, dim), v, cut(upper, at, at + w, dim)], dim)
        wide.append(jnp.pad(joined, pads))
        at += w
    return wide


def strip(values):
    return values[1:-1, 1:-1]


def one_step(padded, conductance, source):
    middle = strip(padded)
    spread = (
        padded[:-2, 1:-1] + padded[2:, 1:-1] + padded[1:-1, :-2] + padded[1:-1, 2:] - 4.0 * middle
    )
    return middle + conductance * spread + source


def line_stats(density):
    rows = density.shape[0]
    mean = jnp.mean(density, axis=0)
    off = density - mean[None]
    stats = jnp.stack([mean, jnp.sum(off * off, axis=0)])
    count = lax.axis_size("py")
    hop = 1
    while hop < count:
        other = lax.ppermute(stats, "py", [(i, i ^ hop) for i in range(count)])
        gap = other[0] - stats[0]
        stats = jnp.stack(
            [
                0.5 * (stats[0] + other[0]),
                stats[1] + other[1] + gap * gap * (0.5 * rows * hop),
            ]
        )
        hop *= 2
    return stats[0], stats[1] / (rows * count)


def per_device(density, conductance, source):
    parts = with_halo(density, conductance, source, "py", 0)
    padded, conductance, source = with_halo(*parts, "px", 1)
    for _ in range(STEPS):
        conductance, source = strip(conductance), strip(source)
        padded = one_step(padded, conductance, source)
    mean, variance = line_stats(padded)
    anomaly = (padded - mean[None]) * lax.rsqrt(variance + 0.0001)[None]
    return (anomaly, padded)


def solution(mesh):
    spec = P("py", "px", None)
    return jax.shard_map(
        per_device, mesh=mesh, in_specs=(spec,) * 3, out_specs=(spec,) * 2, check_vma=False
    )
```

time: 109 us -> 49.1 us (0.45)
  blocking collectives: 67.8 us -> 0 us
  waiting for transfers between devices: 11.5 us -> 20.9 us
  starting transfers between devices: 20.8 us -> 18.3 us
    psum x2 -> x0, blocking collectives: 67.8 us -> none  [the longest x1 34.8 us: per_device(): line_mean = lax.psum(jnp.sum(density, axis=0, keepdims=True), 'py') / count]
    ppermute x8 -> x7, waiting for transfers between devices: 11.5 us -> 20.9 us  [the longest x2 8.68 us: exchange(): lax.ppermute(to_upper, axis, up)]
    ppermute x8 -> x7, starting transfers between devices: 20.8 us -> 18.3 us  [the longest x3 6.84 us: line_stats(): other = lax.ppermute(stats, 'py', [(i, i ^ hop) for i in range(count)])]
    select_n x5 -> x0, other arithmetic: 2.55 us -> none  [per_device(): values = jnp.where(keep_cells.reshape((-1,) + (1,) * 1), values, 0.0)]
    add x0 -> x5, other arithmetic: none -> 2.21 us  [one_step(): return middle + conductance * spread + source]
    slice x3 -> x12, local copies, waits for them, and re-layouts: 0.07 us -> 2.23 us  [cut(): return lax.slice_in_dim(values, start, stop, axis=dim)]
  transfers between devices with their start and end apart: 8 -> 7, of which waited for: 4 -> 7; matrix products, arithmetic and copies ran while one was open for 0% -> 0% of each run, Pallas kernels for 0% -> 0%
where the time goes in v1:
time: 49.1 us; the launch traced here: 48.3 us
  waiting for transfers between devices  20.9 us (43%)
  starting transfers between devices  18.3 us (37%)
  other arithmetic  4.14 us (8%)
  local copies, waits for them, and re-layouts  4.09 us (8%)
  between operations  0.88 us (2%)
    ppermute x2, waiting for transfers between devices, exchange(): lax.ppermute(to_upper, axis, up)  8.68 us
    ppermute x3, starting transfers between devices, line_stats(): other = lax.ppermute(stats, 'py', [(i, i ^ hop) for i in range(count)])  6.84 us
    ppermute x2, starting transfers between devices, exchange(): lax.ppermute(to_upper, axis, up)  6.49 us
    ppermute x3, waiting for transfers between devices, line_stats(): other = lax.ppermute(stats, 'py', [(i, i ^ hop) for i in range(count)])  6.46 us
    ppermute x2, waiting for transfers between devices, exchange(): lax.ppermute(to_lower, axis, down)  5.76 us
    ppermute x2, starting transfers between devices, exchange(): lax.ppermute(to_lower, axis, down)  4.93 us
    slice x12, local copies, waits for them, and re-layouts, cut(): return lax.slice_in_dim(values, start, stop, axis=dim)  2.23 us
    add x5, other arithmetic, one_step(): return middle + conductance * spread + source  2.21 us
  transfers between devices with their start and end apart: 7, of which 7 were waited for; matrix products, arithmetic and copies ran while one was open for 0% of the time, Pallas kernels for 0%

profile of v1, /device:TPU:4, one launch (start us, length us, event | category | flops | bytes accessed | tf_op | source)
XLA Modules:
  0.0 48.3 jit_solution(9931519247517546318)
XLA Ops:
  0.6 1.0 %fusion.36 = (f32[6,32,128]{2,1,0:T(8,128)S(1)}, f32[6,32,128]{2,1,0:T(8,128)S(1)}) fusion(f32[32,32,128]{2,1,0:T(8,128)} %param.3), kind=kLoop, calls=%fused_computation.86 | loop fusion | bytes 393216 | tf_op jit(solution)/shard_map/slice | solution.py:17
  1.6 0.0 copy-start.3
  1.6 1.1 %fusion.37 = (f32[5,32,128]{2,1,0:T(8,128)S(1)}, f32[5,32,128]{2,1,0:T(8,128)S(1)}, f32[5,32,128]{2,1,0:T(8,128)S(1)}, f32[5,32,128]{2,1,0:T(8,128)S(1)}) fusion(f32[32,32,128]{2,1,0:T(8,128)} %param.4, f32[32,32,128]{2,1,0:T(8,128)} %param.5), kind=kLoop, calls=%fused_computation.87 | loop fusion | bytes 655360 | tf_op jit(solution)/shard_map/slice | solution.py:17
  2.7 1.3 %collective-permute-start.1 = (f32[16,32,128]{2,1,0:T(8,128)S(1)}, f32[16,32,128]{2,1,0:T(8,128)S(1)}, u32[]{:S(2)}, u32[]{:S(2)}) collective-permute-start(f32[16,32,128]{2,1,0:T(8,128)S(1)} %pad_maximum_fusion.6), channel_id=1, source_target_pairs={{4,0},{8,4},{12,8},{16,12},{20,16},{24,20},{28,24},{5,1},{9,5},{13... | collective-permute-start | bytes 786440 | tf_op jit(solution)/shard_map/ppermute | solution.py:13
  4.0 4.6 %collective-permute-start = (f32[16,32,128]{2,1,0:T(8,128)S(1)}, f32[16,32,128]{2,1,0:T(8,128)S(1)}, u32[]{:S(2)}, u32[]{:S(2)}) collective-permute-start(f32[16,32,128]{2,1,0:T(8,128)S(1)} %pad_maximum_fusion.5), channel_id=1, source_target_pairs={{0,4},{4,8},{8,12},{12,16},{16,20},{20,24},{24,28},{1,5},{5,9},{9,... | collective-permute-start | bytes 786440 | tf_op jit(solution)/shard_map/ppermute | solution.py:13
  8.6 4.0 %collective-permute-done.1 = f32[16,32,128]{2,1,0:T(8,128)S(1)} collective-permute-done((f32[16,32,128]{2,1,0:T(8,128)S(1)}, f32[16,32,128]{2,1,0:T(8,128)S(1)}, u32[]{:S(2)}, u32[]{:S(2)}) %collective-permute-start.1) | collective-permute-done | bytes 262176 | tf_op jit(solution)/shard_map/ppermute | solution.py:13
  12.7 5.5 %collective-permute-done = f32[16,32,128]{2,1,0:T(8,128)S(1)} collective-permute-done((f32[16,32,128]{2,1,0:T(8,128)S(1)}, f32[16,32,128]{2,1,0:T(8,128)S(1)}, u32[]{:S(2)}, u32[]{:S(2)}) %collective-permute-start) | collective-permute-done | bytes 262176 | tf_op jit(solution)/shard_map/ppermute | solution.py:13
  18.2 0.0 copy-start.2
  18.2 0.0 copy-done.3
  18.3 0.9 %copy-done.2 = f32[32,32,128]{2,1,0:T(8,128)S(1)} copy-done((f32[32,32,128]{2,1,0:T(8,128)S(1)}, f32[32,32,128]{2,1,0:T(8,128)}, u32[]{:S(2)}) %copy-start.2) | copy-done | bytes 524312
  19.2 0.0 copy-start.1
  19.4 0.9 %copy-done.1 = f32[32,32,128]{2,1,0:T(8,128)S(1)} copy-done((f32[32,32,128]{2,1,0:T(8,128)S(1)}, f32[32,32,128]{2,1,0:T(8,128)}, u32[]{:S(2)}) %copy-start.1) | copy-done | bytes 524312
  20.3 0.1 fusion.23
  20.4 1.9 %collective-permute-start.2 = (f32[44,16,128]{2,1,0:T(8,128)S(1)}, f32[44,16,128]{2,1,0:T(8,128)S(1)}, u32[]{:S(2)}, u32[]{:S(2)}) collective-permute-start(f32[44,16,128]{2,1,0:T(8,128)S(1)} %get-tuple-element.4), channel_id=1, source_target_pairs={{0,1},{1,2},{2,3},{4,5},{5,6},{6,7},{8,9},{9,10},{10,11},{12,13},{... | collective-permute-start | bytes 1081352 | tf_op jit(solution)/shard_map/ppermute | solution.py:13
  22.4 3.6 %collective-permute-start.3 = (f32[44,16,128]{2,1,0:T(8,128)S(1)}, f32[44,16,128]{2,1,0:T(8,128)S(1)}, u32[]{:S(2)}, u32[]{:S(2)}) collective-permute-start(f32[44,16,128]{2,1,0:T(8,128)S(1)} %get-tuple-element.5), channel_id=1, source_target_pairs={{1,0},{2,1},{3,2},{5,4},{6,5},{7,6},{9,8},{10,9},{11,10},{13,12},{... | collective-permute-start | bytes 1081352 | tf_op jit(solution)/shard_map/ppermute | solution.py:13
  26.0 3.2 %collective-permute-done.2 = f32[44,16,128]{2,1,0:T(8,128)S(1)} collective-permute-done((f32[44,16,128]{2,1,0:T(8,128)S(1)}, f32[44,16,128]{2,1,0:T(8,128)S(1)}, u32[]{:S(2)}, u32[]{:S(2)}) %collective-permute-start.2) | collective-permute-done | bytes 360480 | tf_op jit(solution)/shard_map/ppermute | solution.py:13
  29.2 1.7 %collective-permute-done.3 = f32[44,16,128]{2,1,0:T(8,128)S(1)} collective-permute-done((f32[44,16,128]{2,1,0:T(8,128)S(1)}, f32[44,16,128]{2,1,0:T(8,128)S(1)}, u32[]{:S(2)}, u32[]{:S(2)}) %collective-permute-start.3) | collective-permute-done | bytes 360480 | tf_op jit(solution)/shard_map/ppermute | solution.py:13
  31.0 0.1 pad_maximum_fusion.1
  31.1 0.1 pad_maximum_fusion.2
  31.3 0.1 pad_maximum_fusion
  31.4 0.4 slice_add_fusion
  31.9 0.4 slice_add_fusion.4
  32.3 0.5 slice_add_fusion.8
  32.8 0.4 slice_add_fusion.12
  33.2 0.4 slice_add_fusion.16
  33.7 0.3 fusion.32
  33.9 0.0 copy-start
  34.0 0.1 multiply_reduce_fusion
  34.0 2.5 %collective-permute-start.4 = (f32[2,32,128]{2,1,0:T(8,128)S(1)}, f32[2,32,128]{2,1,0:T(8,128)S(1)}, u32[]{:S(2)}, u32[]{:S(2)}) collective-permute-start(f32[2,32,128]{2,1,0:T(8,128)S(1)} %pad_maximum_fusion.7), channel_id=1, source_target_pairs={{0,4},{4,0},{8,12},{12,8},{16,20},{20,16},{24,28},{28,24},{1,5},{5... | collective-permute-start | bytes 98312 | tf_op jit(solution)/shard_map/ppermute | solution.py:59
  36.6 1.9 %collective-permute-done.4 = f32[2,32,128]{2,1,0:T(8,128)S(1)} collective-permute-done((f32[2,32,128]{2,1,0:T(8,128)S(1)}, f32[2,32,128]{2,1,0:T(8,128)S(1)}, u32[]{:S(2)}, u32[]{:S(2)}) %collective-permute-start.4) | collective-permute-done | bytes 32800 | tf_op jit(solution)/shard_map/ppermute | solution.py:59
  38.5 1.6 %collective-permute-start.5 = (f32[2,32,128]{2,1,0:T(8,128)S(1)}, f32[2,32,128]{2,1,0:T(8,128)S(1)}, u32[]{:S(2)}, u32[]{:S(2)}) collective-permute-start(f32[2,32,128]{2,1,0:T(8,128)S(1)} %pad_maximum_fusion.8), channel_id=1, source_target_pairs={{0,8},{4,12},{8,0},{12,4},{16,24},{20,28},{24,16},{28,20},{1,9},{5... | collective-permute-start | bytes 98312 | tf_op jit(solution)/shard_map/ppermute | solution.py:59
  40.1 2.3 %collective-permute-done.5 = f32[2,32,128]{2,1,0:T(8,128)S(1)} collective-permute-done((f32[2,32,128]{2,1,0:T(8,128)S(1)}, f32[2,32,128]{2,1,0:T(8,128)S(1)}, u32[]{:S(2)}, u32[]{:S(2)}) %collective-permute-start.5) | collective-permute-done | bytes 32800 | tf_op jit(solution)/shard_map/ppermute | solution.py:59
  42.5 2.7 %collective-permute-start.6 = (f32[2,32,128]{2,1,0:T(8,128)S(1)}, f32[2,32,128]{2,1,0:T(8,128)S(1)}, u32[]{:S(2)}, u32[]{:S(2)}) collective-permute-start(f32[2,32,128]{2,1,0:T(8,128)S(1)} %pad_maximum_fusion.9), channel_id=1, source_target_pairs={{0,16},{4,20},{8,24},{12,28},{16,0},{20,4},{24,8},{28,12},{1,17},{... | collective-permute-start | bytes 98312 | tf_op jit(solution)/shard_map/ppermute | solution.py:59
  45.2 2.2 %collective-permute-done.6 = f32[2,32,128]{2,1,0:T(8,128)S(1)} collective-permute-done((f32[2,32,128]{2,1,0:T(8,128)S(1)}, f32[2,32,128]{2,1,0:T(8,128)S(1)}, u32[]{:S(2)}, u32[]{:S(2)}) %collective-permute-start.6) | collective-permute-done | bytes 32800 | tf_op jit(solution)/shard_map/ppermute | solution.py:59
  47.4 0.9 %subtract_multiply_fusion = f32[32,32,128]{2,1,0:T(8,128)} fusion(f32[32,32,128]{2,1,0:T(8,128)S(1)} %get-tuple-element.3, f32[32,128]{1,0:T(8,128)S(1)} %get-tuple-element.25, f32[32,128]{1,0:T(8,128)S(1)} %get-tuple-element.24), kind=kLoop, calls=%fused_computation.52 | loop fusion | flops 262144 | bytes 1081344 | tf_op jit(solution)/shard_map/mul | solution.py:78
  48.3 0.0 copy-done
  (21 shorter events, 0.4 us)
Async XLA Ops:
  1.6 16.6 %copy-start.3 = (f32[32,32,128]{2,1,0:T(8,128)S(1)}, f32[32,32,128]{2,1,0:T(8,128)}, u32[]{:S(2)}) copy-start(f32[32,32,128]{2,1,0:T(8,128)} %param.4) | copy-start | bytes 1572868
  2.7 9.9 %collective-permute-start.1 = (f32[16,32,128]{2,1,0:T(8,128)S(1)}, f32[16,32,128]{2,1,0:T(8,128)S(1)}, u32[]{:S(2)}, u32[]{:S(2)}) collective-permute-start(f32[16,32,128]{2,1,0:T(8,128)S(1)} %pad_maximum_fusion.6), channel_id=1, source_target_pairs={{4,0},{8,4},{12,8},{16,12},{20,16},{24,20},{28,24},{5,1},{9,5},{13... | collective-permute-start | bytes 786440 | tf_op jit(solution)/shard_map/ppermute | solution.py:13
  4.0 14.1 %collective-permute-start = (f32[16,32,128]{2,1,0:T(8,128)S(1)}, f32[16,32,128]{2,1,0:T(8,128)S(1)}, u32[]{:S(2)}, u32[]{:S(2)}) collective-permute-start(f32[16,32,128]{2,1,0:T(8,128)S(1)} %pad_maximum_fusion.5), channel_id=1, source_target_pairs={{0,4},{4,8},{8,12},{12,16},{16,20},{20,24},{24,28},{1,5},{5,9},{9,... | collective-permute-start | bytes 786440 | tf_op jit(solution)/shard_map/ppermute | solution.py:13
  18.2 1.0 %copy-start.2 = (f32[32,32,128]{2,1,0:T(8,128)S(1)}, f32[32,32,128]{2,1,0:T(8,128)}, u32[]{:S(2)}) copy-start(f32[32,32,128]{2,1,0:T(8,128)} %param.5) | copy-start | bytes 1572868
  19.2 1.0 %copy-start.1 = (f32[32,32,128]{2,1,0:T(8,128)S(1)}, f32[32,32,128]{2,1,0:T(8,128)}, u32[]{:S(2)}) copy-start(f32[32,32,128]{2,1,0:T(8,128)} %param.3) | copy-start | bytes 1572868
  20.4 8.7 %collective-permute-start.2 = (f32[44,16,128]{2,1,0:T(8,128)S(1)}, f32[44,16,128]{2,1,0:T(8,128)S(1)}, u32[]{:S(2)}, u32[]{:S(2)}) collective-permute-start(f32[44,16,128]{2,1,0:T(8,128)S(1)} %get-tuple-element.4), channel_id=1, source_target_pairs={{0,1},{1,2},{2,3},{4,5},{5,6},{6,7},{8,9},{9,10},{10,11},{12,13},{... | collective-permute-start | bytes 1081352 | tf_op jit(solution)/shard_map/ppermute | solution.py:13
  22.4 8.6 %collective-permute-start.3 = (f32[44,16,128]{2,1,0:T(8,128)S(1)}, f32[44,16,128]{2,1,0:T(8,128)S(1)}, u32[]{:S(2)}, u32[]{:S(2)}) collective-permute-start(f32[44,16,128]{2,1,0:T(8,128)S(1)} %get-tuple-element.5), channel_id=1, source_target_pairs={{1,0},{2,1},{3,2},{5,4},{6,5},{7,6},{9,8},{10,9},{11,10},{13,12},{... | collective-permute-start | bytes 1081352 | tf_op jit(solution)/shard_map/ppermute | solution.py:13
  33.9 14.3 %copy-start = (f32[32,32,128]{2,1,0:T(8,128)}, f32[32,32,128]{2,1,0:T(8,128)S(1)}, u32[]{:S(2)}) copy-start(f32[32,32,128]{2,1,0:T(8,128)S(1)} %get-tuple-element.3) | copy-start | bytes 1572868
  34.0 4.4 %collective-permute-start.4 = (f32[2,32,128]{2,1,0:T(8,128)S(1)}, f32[2,32,128]{2,1,0:T(8,128)S(1)}, u32[]{:S(2)}, u32[]{:S(2)}) collective-permute-start(f32[2,32,128]{2,1,0:T(8,128)S(1)} %pad_maximum_fusion.7), channel_id=1, source_target_pairs={{0,4},{4,0},{8,12},{12,8},{16,20},{20,16},{24,28},{28,24},{1,5},{5... | collective-permute-start | bytes 98312 | tf_op jit(solution)/shard_map/ppermute | solution.py:59
  38.5 4.0 %collective-permute-start.5 = (f32[2,32,128]{2,1,0:T(8,128)S(1)}, f32[2,32,128]{2,1,0:T(8,128)S(1)}, u32[]{:S(2)}, u32[]{:S(2)}) collective-permute-start(f32[2,32,128]{2,1,0:T(8,128)S(1)} %pad_maximum_fusion.8), channel_id=1, source_target_pairs={{0,8},{4,12},{8,0},{12,4},{16,24},{20,28},{24,16},{28,20},{1,9},{5... | collective-permute-start | bytes 98312 | tf_op jit(solution)/shard_map/ppermute | solution.py:59
  42.5 4.9 %collective-permute-start.6 = (f32[2,32,128]{2,1,0:T(8,128)S(1)}, f32[2,32,128]{2,1,0:T(8,128)S(1)}, u32[]{:S(2)}, u32[]{:S(2)}) collective-permute-start(f32[2,32,128]{2,1,0:T(8,128)S(1)} %pad_maximum_fusion.9), channel_id=1, source_target_pairs={{0,16},{4,20},{8,24},{12,28},{16,0},{20,4},{24,8},{28,12},{1,17},{... | collective-permute-start | bytes 98312 | tf_op jit(solution)/shard_map/ppermute | solution.py:59
